TPU v7x, 32 devices: a whole 2x2x4 slice. The times are simulated.
32 devices in a mesh: ta: 2 (over x), gz: 4 (over z), xy: 4 (over y, core).
Axes of the slice: x: 2, y: 2, z: 4, core: 2. Of those that a mesh axis runs over, the one named last changes fastest.
Arguments:
- source: float32 [2, 48, 2, 4, 512], P(None, None, 'ta', 'gz', 'xy'), may hold values from -14 to 14
- inverse: bfloat16 [2, 48, 48, 2, 4, 512], P(None, None, None, 'ta', 'gz', 'xy'), may hold values from -0.625 to 0.625
- coarse_links: bfloat16 [8, 2, 48, 48, 2, 4, 512], P(None, None, None, None, 'ta', 'gz', 'xy'), may hold values from -0.15625 to 0.15625
Outputs:
- solution: float32 [2, 48, 2, 4, 512], P(None, None, 'ta', 'gz', 'xy')
- residual: float32 [2, 48, 2, 4, 512], P(None, None, 'ta', 'gz', 'xy')
- hessenberg: float32 [2, 6, 5], replicated
All inputs are finite; a program needn't handle non-finite values.
Results may differ from a plain program's by a relative error of at most 0.0003.
Values sent between devices are 32-bit elements; how exact they have to be, the bound alone decides.
A program may use at most 128 MiB of HBM per device.

v0:
```python
import jax
import jax.numpy as jnp
from jax import lax
from jax.sharding import PartitionSpec as P

LY = 16
ITERS = 5


def padded_2(cells, sides, width):
    for axis, dim in sides:
        count = lax.axis_size(axis)
        head = lax.slice_in_dim(cells, 0, width, axis=dim)
        tail = lax.slice_in_dim(cells, cells.shape[dim] - width, cells.shape[dim], axis=dim)
        cells = jnp.concatenate(
            [
                lax.ppermute(tail, axis, [(i, (i + 1) % count) for i in range(count)]),
                cells,
                lax.ppermute(head, axis, [((i + 1) % count, i) for i in range(count)]),
            ],
            axis=dim,
        )
    return cells


def block_apply(blocks, vector):
    real_blocks = blocks[0].astype(jnp.float32)
    imag_blocks = blocks[1].astype(jnp.float32)
    vec_real = vector[0][None]
    vec_imag = vector[1][None]
    real_part = jnp.sum(real_blocks * vec_real - imag_blocks * vec_imag, axis=1)
    imag_part = jnp.sum(real_blocks * vec_imag + imag_blocks * vec_real, axis=1)
    return jnp.stack([real_part, imag_part])


def complex_dot(left, right):
    real_part = jnp.sum(left[0] * right[0] + left[1] * right[1])
    imag_part = jnp.sum(left[0] * right[1] - left[1] * right[0])
    return (real_part, imag_part)


def scaled(coef_real, coef_imag, vector):
    return jnp.stack(
        [
            coef_real * vector[0] - coef_imag * vector[1],
            coef_real * vector[1] + coef_imag * vector[0],
        ]
    )


def y_neighbours(field):
    positions = jnp.arange(field.shape[4]) % LY
    is_last = positions == LY - 1
    is_first = positions == 0
    forward = jnp.where(is_last, jnp.roll(field, LY - 1, axis=4), jnp.roll(field, -1, axis=4))
    backward = jnp.where(is_first, jnp.roll(field, 1 - LY, axis=4), jnp.roll(field, 1, axis=4))
    return (forward, backward)


def apply_operator(field, inverse, coarse_links):
    padded = padded_2(field, (("ta", 2), ("gz", 3)), 1)
    widened = padded_2(field, (("xy", 4),), LY)
    extent = field.shape[4]
    forward_y, backward_y = y_neighbours(field)
    neighbours = [
        padded[:, :, 2:, 1:-1],
        padded[:, :, :-2, 1:-1],
        padded[:, :, 1:-1, 2:],
        padded[:, :, 1:-1, :-2],
        widened[..., 2 * LY : 2 * LY + extent],
        widened[..., :extent],
        forward_y,
        backward_y,
    ]
    hopping = block_apply(coarse_links[0], neighbours[0])
    for d in range(1, 8):
        hopping = hopping + block_apply(coarse_links[d], neighbours[d])
    return field + block_apply(inverse, hopping)


def solve_small(hessenberg, source_norm):
    upper_half = jnp.concatenate([hessenberg[0], -hessenberg[1]], axis=1)
    lower_half = jnp.concatenate([hessenberg[1], hessenberg[0]], axis=1)
    real_form = jnp.concatenate([upper_half, lower_half], axis=0)
    target = jnp.zeros((2 * (ITERS + 1),), jnp.float32).at[0].set(source_norm)
    normal_mat = jnp.dot(real_form.T, real_form, precision=lax.Precision.HIGHEST)
    projected = jnp.dot(real_form.T, target, precision=lax.Precision.HIGHEST)
    factor = jnp.linalg.cholesky(normal_mat)
    forward_vals = []
    for i in range(2 * ITERS):
        partial_sum = projected[i]
        for k in range(i):
            partial_sum = partial_sum - factor[i, k] * forward_vals[k]
        forward_vals.append(partial_sum / factor[i, i])
    solved = [None] * (2 * ITERS)
    for i in reversed(range(2 * ITERS)):
        partial_sum = forward_vals[i]
        for k in range(i + 1, 2 * ITERS):
            partial_sum = partial_sum - factor[k, i] * solved[k]
        solved[i] = partial_sum / factor[i, i]
    coeffs = jnp.stack(solved)
    return (coeffs[:ITERS], coeffs[ITERS:], target)


def per_device(source, inverse, coarse_links):
    norm_sq = lax.psum(complex_dot(source, source)[0], ("ta", "gz", "xy"))
    source_norm = jnp.sqrt(norm_sq)
    krylov_basis = [source / source_norm]
    hessenberg = jnp.zeros((2, ITERS + 1, ITERS), jnp.float32)
    for j in range(ITERS):
        candidate = apply_operator(krylov_basis[j], inverse, coarse_links)
        local_pairs = [complex_dot(krylov_basis[i], candidate) for i in range(j + 1)]
        whole_local = complex_dot(candidate, candidate)[0]
        proj_reals, proj_imags, whole_sq = lax.psum(
            (
                jnp.stack([entry[0] for entry in local_pairs]),
                jnp.stack([entry[1] for entry in local_pairs]),
                whole_local,
            ),
            ("ta", "gz", "xy"),
        )
        for i in range(j + 1):
            candidate = candidate - scaled(proj_reals[i], proj_imags[i], krylov_basis[i])
            hessenberg = hessenberg.at[0, i, j].set(proj_reals[i]).at[1, i, j].set(proj_imags[i])
        length_sq = whole_sq - jnp.sum(proj_reals * proj_reals + proj_imags * proj_imags)
        length = jnp.sqrt(length_sq)
        hessenberg = hessenberg.at[0, j + 1, j].set(length)
        krylov_basis.append(candidate / length)
    coef_real, coef_imag, target = solve_small(hessenberg, source_norm)
    solution = scaled(coef_real[0], coef_imag[0], krylov_basis[0])
    for j in range(1, ITERS):
        solution = solution + scaled(coef_real[j], coef_imag[j], krylov_basis[j])
    residual = source - apply_operator(solution, inverse, coarse_links)
    return (solution, residual, hessenberg)


def solution(mesh):
    return jax.shard_map(
        per_device,
        mesh=mesh,
        in_specs=(
            P(None, None, "ta", "gz", "xy"),
            P(None, None, None, "ta", "gz", "xy"),
            P(None, None, None, None, "ta", "gz", "xy"),
        ),
        out_specs=(P(None, None, "ta", "gz", "xy"), P(None, None, "ta", "gz", "xy"), P()),
        check_vma=False,
    )
```

profile of v0, /device:TPU:0, one launch (start us, length us, event | category | flops | bytes accessed | tf_op | source)
XLA Modules:
  0.0 561.9 jit_solution(17427624493626627391)
XLA Ops:
  2.1 42.2 %psum.112 = f32[]{:T(128)} all-reduce(f32[]{:T(128)} %add_reduce_fusion.20), channel_id=1, replica_groups=mesh['ta'=2,'gz'=4,'xy'=4] {'ta','gz','xy'}, use_global_device_ids=true, to_apply=%region_1.0 | all-reduce | flops 1 | bytes 8 | tf_op jit(solution)/shard_map/psum | solution.py:106
  45.8 2.3 collective-permute-start
  53.1 3.7 fusion.169
  57.0 2.3 collective-permute-start.2
  59.2 3.0 fusion.25
  63.5 4.9 collective-permute-done.3
  68.4 3.8 fusion.97
  73.8 38.8 %all-reduce.6 = (f32[1]{0:T(128)}, f32[1]{0:T(128)}, f32[]{:T(128)}) all-reduce(f32[1]{0:T(128)} %bitcast.81, f32[1]{0:T(128)} %bitcast.83, f32[]{:T(128)} %get-tuple-element.653), channel_id=1, replica_groups=mesh['ta'=2,'gz'=4,'xy'=4] {'ta','gz','xy'}, use_global_device_ids=true, to_apply=%region_21.22 | all-reduce | flops 3 | bytes 24 | tf_op jit(solution)/shard_map/psum | solution.py:114
  118.2 2.3 collective-permute-start.6
  125.7 3.7 fusion.173
  131.1 2.3 collective-permute-start.8
  133.4 3.0 fusion.29
  139.9 3.7 fusion.101
  148.0 38.8 %all-reduce.5 = (f32[2]{0:T(128)S(1)}, f32[2]{0:T(128)S(1)}, f32[]{:T(128)}) all-reduce(f32[2]{0:T(128)S(1)} %pad_maximum_fusion.30, f32[2]{0:T(128)S(1)} %pad_maximum_fusion.31, f32[]{:T(128)} %get-tuple-element.650), channel_id=1, replica_groups=mesh['ta'=2,'gz'=4,'xy'=4] {'ta','gz','xy'}, use_global_device_ids=true, to_apply=%region_46.47 | all-reduce | flops 5 | bytes 40 | tf_op jit(solution)/shard_map/psum | solution.py:114
  193.7 2.3 collective-permute-start.12
  201.3 3.7 fusion.177
  207.2 3.0 fusion.33
  211.1 4.2 collective-permute-done.15
  215.3 3.7 fusion.105
  220.8 2.0 pad_maximum_fusion.33
  224.6 39.9 %all-reduce.4 = (f32[3]{0:T(128)S(1)}, f32[3]{0:T(128)S(1)}, f32[]{:T(128)}) all-reduce(f32[3]{0:T(128)S(1)} %pad_maximum_fusion.32, f32[3]{0:T(128)S(1)} %pad_maximum_fusion.33, f32[]{:T(128)} %get-tuple-element.647), channel_id=1, replica_groups=mesh['ta'=2,'gz'=4,'xy'=4] {'ta','gz','xy'}, use_global_device_ids=true, to_apply=%region_74.75 | all-reduce | flops 7 | bytes 56 | tf_op jit(solution)/shard_map/psum | solution.py:114
  272.8 2.3 collective-permute-start.18
  277.9 2.7 scatter.136
  283.6 3.7 fusion.181
  287.4 2.1 collective-permute-start.20
  289.5 3.0 fusion.37
  293.4 4.6 collective-permute-done.21
  298.1 3.7 fusion.109
  303.7 2.6 pad_maximum_fusion.35
  306.3 2.6 pad_maximum_fusion.34
  308.8 39.9 %all-reduce.3 = (f32[4]{0:T(128)S(1)}, f32[4]{0:T(128)S(1)}, f32[]{:T(128)}) all-reduce(f32[4]{0:T(128)S(1)} %pad_maximum_fusion.34, f32[4]{0:T(128)S(1)} %pad_maximum_fusion.35, f32[]{:T(128)} %get-tuple-element.642), channel_id=1, replica_groups=mesh['ta'=2,'gz'=4,'xy'=4] {'ta','gz','xy'}, use_global_device_ids=true, to_apply=%region_104.105 | all-reduce | flops 9 | bytes 72 | tf_op jit(solution)/shard_map/psum | solution.py:114
  358.5 2.3 collective-permute-start.24
  368.9 3.7 fusion.185
  372.8 2.1 collective-permute-start.26
  374.9 3.0 fusion.41
  378.7 4.4 collective-permute-done.27
  383.2 3.7 fusion.113
  389.1 3.2 stack.868
  392.3 3.3 stack.862
  395.6 40.1 %all-reduce.2 = (f32[5]{0:T(128)S(1)}, f32[5]{0:T(128)S(1)}, f32[]{:T(128)}) all-reduce(f32[5]{0:T(128)S(1)} %stack.862, f32[5]{0:T(128)S(1)} %stack.868, f32[]{:T(128)} %get-tuple-element.751), channel_id=1, replica_groups=mesh['ta'=2,'gz'=4,'xy'=4] {'ta','gz','xy'}, use_global_device_ids=true, to_apply=%region_136.137 | all-reduce | flops 11 | bytes 88 | tf_op jit(solution)/shard_map/psum | solution.py:114
  442.2 2.5 dynamic-slice.250
  446.5 2.0 scatter.166
  535.3 2.3 collective-permute-start.30
  539.9 2.6 collective-permute-done.35
  542.8 3.7 fusion.189
  548.8 3.0 fusion.45
  552.8 3.5 collective-permute-done.33
  556.3 3.7 fusion.117
  (274 shorter events, 103.5 us)
Async XLA Ops:
  0.6 50.9 %copy-start.3 = (s32[3]{0:T(128)S(1)}, s32[3]{0:T(128)}, u32[]{:S(2)}) copy-start(s32[3]{0:T(128)} %constant.1127.clone.1) | copy-start | bytes 40
  45.8 11.1 %collective-permute-start = (f32[2,48,1,1,128]{4,3,2,1,0:T(1,128)S(1)}, f32[2,48,1,1,128]{4,3,2,1,0:T(1,128)S(1)}, u32[]{:S(2)}, u32[]{:S(2)}) collective-permute-start(f32[2,48,1,1,128]{4,3,2,1,0:T(1,128)S(1)} %broadcast_divide_fusion), channel_id=1, source_target_pairs={{16,0},{0,16},{17,1},{1,17},{18,2},{2,18},{19,3},{3,19},{20,4},{4,... | collective-permute-start | bytes 147464 | tf_op jit(solution)/shard_map/ppermute | solution.py:19
  48.1 8.7 %collective-permute-start.1 = (f32[2,48,1,1,128]{4,3,2,1,0:T(1,128)S(1)}, f32[2,48,1,1,128]{4,3,2,1,0:T(1,128)S(1)}, u32[]{:S(2)}, u32[]{:S(2)}) collective-permute-start(f32[2,48,1,1,128]{4,3,2,1,0:T(1,128)S(1)} %broadcast_divide_fusion), channel_id=1, source_target_pairs={{0,16},{16,0},{1,17},{17,1},{2,18},{18,2},{3,19},{19,3},{4,20},{20... | collective-permute-start | bytes 147464 | tf_op jit(solution)/shard_map/ppermute | solution.py:17
  48.3 3.9 collective-permute-start.4
  48.4 4.4 collective-permute-start.5
  57.0 6.5 %collective-permute-start.2 = (f32[2,48,3,1,128]{4,3,2,1,0:T(1,128)S(1)}, f32[2,48,3,1,128]{4,3,2,1,0:T(1,128)S(1)}, u32[]{:S(2)}, u32[]{:S(2)}) collective-permute-start(f32[2,48,3,1,128]{4,3,2,1,0:T(1,128)S(1)} %pad_maximum_fusion), channel_id=1, source_target_pairs={{4,0},{8,4},{12,8},{0,12},{5,1},{9,5},{13,9},{1,13},{6,2},{10,6},{... | collective-permute-start | bytes 442376 | tf_op jit(solution)/shard_map/ppermute | solution.py:19
  59.2 9.1 %collective-permute-start.3 = (f32[2,48,3,1,128]{4,3,2,1,0:T(1,128)S(1)}, f32[2,48,3,1,128]{4,3,2,1,0:T(1,128)S(1)}, u32[]{:S(2)}, u32[]{:S(2)}) collective-permute-start(f32[2,48,3,1,128]{4,3,2,1,0:T(1,128)S(1)} %pad_maximum_fusion), channel_id=1, source_target_pairs={{0,4},{4,8},{8,12},{12,0},{1,5},{5,9},{9,13},{13,1},{2,6},{6,10},{... | collective-permute-start | bytes 442376 | tf_op jit(solution)/shard_map/ppermute | solution.py:17
  68.4 3.8 copy-start
  72.2 0.8 copy-start.2
  118.2 11.2 %collective-permute-start.6 = (f32[2,48,1,1,128]{4,3,2,1,0:T(1,128)S(1)}, f32[2,48,1,1,128]{4,3,2,1,0:T(1,128)S(1)}, u32[]{:S(2)}, u32[]{:S(2)}) collective-permute-start(f32[2,48,1,1,128]{4,3,2,1,0:T(1,128)S(1)} %fusion.222), channel_id=1, source_target_pairs={{16,0},{0,16},{17,1},{1,17},{18,2},{2,18},{19,3},{3,19},{20,4},{4,... | collective-permute-start | bytes 147464 | tf_op jit(solution)/shard_map/ppermute | solution.py:19
  120.5 8.9 %collective-permute-start.7 = (f32[2,48,1,1,128]{4,3,2,1,0:T(1,128)S(1)}, f32[2,48,1,1,128]{4,3,2,1,0:T(1,128)S(1)}, u32[]{:S(2)}, u32[]{:S(2)}) collective-permute-start(f32[2,48,1,1,128]{4,3,2,1,0:T(1,128)S(1)} %fusion.222), channel_id=1, source_target_pairs={{0,16},{16,0},{1,17},{17,1},{2,18},{18,2},{3,19},{19,3},{4,20},{20... | collective-permute-start | bytes 147464 | tf_op jit(solution)/shard_map/ppermute | solution.py:17
  120.9 2.5 collective-permute-start.10
  121.0 4.4 collective-permute-start.11
  129.6 8.6 %collective-permute-start.9 = (f32[2,48,3,1,128]{4,3,2,1,0:T(1,128)S(1)}, f32[2,48,3,1,128]{4,3,2,1,0:T(1,128)S(1)}, u32[]{:S(2)}, u32[]{:S(2)}) collective-permute-start(f32[2,48,3,1,128]{4,3,2,1,0:T(1,128)S(1)} %pad_maximum_fusion.1), channel_id=1, source_target_pairs={{0,4},{4,8},{8,12},{12,0},{1,5},{5,9},{9,13},{13,1},{2,6},{6,10},{... | collective-permute-start | bytes 442376 | tf_op jit(solution)/shard_map/ppermute | solution.py:17
  131.1 8.8 %collective-permute-start.8 = (f32[2,48,3,1,128]{4,3,2,1,0:T(1,128)S(1)}, f32[2,48,3,1,128]{4,3,2,1,0:T(1,128)S(1)}, u32[]{:S(2)}, u32[]{:S(2)}) collective-permute-start(f32[2,48,3,1,128]{4,3,2,1,0:T(1,128)S(1)} %pad_maximum_fusion.1), channel_id=1, source_target_pairs={{4,0},{8,4},{12,8},{0,12},{5,1},{9,5},{13,9},{1,13},{6,2},{10,6},{... | collective-permute-start | bytes 442376 | tf_op jit(solution)/shard_map/ppermute | solution.py:19
  193.7 11.3 %collective-permute-start.12 = (f32[2,48,1,1,128]{4,3,2,1,0:T(1,128)S(1)}, f32[2,48,1,1,128]{4,3,2,1,0:T(1,128)S(1)}, u32[]{:S(2)}, u32[]{:S(2)}) collective-permute-start(f32[2,48,1,1,128]{4,3,2,1,0:T(1,128)S(1)} %fusion.262), channel_id=1, source_target_pairs={{16,0},{0,16},{17,1},{1,17},{18,2},{2,18},{19,3},{3,19},{20,4},{4,... | collective-permute-start | bytes 147464 | tf_op jit(solution)/shard_map/ppermute | solution.py:19
  196.0 9.0 %collective-permute-start.13 = (f32[2,48,1,1,128]{4,3,2,1,0:T(1,128)S(1)}, f32[2,48,1,1,128]{4,3,2,1,0:T(1,128)S(1)}, u32[]{:S(2)}, u32[]{:S(2)}) collective-permute-start(f32[2,48,1,1,128]{4,3,2,1,0:T(1,128)S(1)} %fusion.262), channel_id=1, source_target_pairs={{0,16},{16,0},{1,17},{17,1},{2,18},{18,2},{3,19},{19,3},{4,20},{20... | collective-permute-start | bytes 147464 | tf_op jit(solution)/shard_map/ppermute | solution.py:17
  196.4 4.5 collective-permute-start.16
  196.5 4.4 collective-permute-start.17
  205.1 5.9 %collective-permute-start.14 = (f32[2,48,3,1,128]{4,3,2,1,0:T(1,128)S(1)}, f32[2,48,3,1,128]{4,3,2,1,0:T(1,128)S(1)}, u32[]{:S(2)}, u32[]{:S(2)}) collective-permute-start(f32[2,48,3,1,128]{4,3,2,1,0:T(1,128)S(1)} %pad_maximum_fusion.2), channel_id=1, source_target_pairs={{4,0},{8,4},{12,8},{0,12},{5,1},{9,5},{13,9},{1,13},{6,2},{10,6},{... | collective-permute-start | bytes 442376 | tf_op jit(solution)/shard_map/ppermute | solution.py:19
  206.8 8.5 %collective-permute-start.15 = (f32[2,48,3,1,128]{4,3,2,1,0:T(1,128)S(1)}, f32[2,48,3,1,128]{4,3,2,1,0:T(1,128)S(1)}, u32[]{:S(2)}, u32[]{:S(2)}) collective-permute-start(f32[2,48,3,1,128]{4,3,2,1,0:T(1,128)S(1)} %pad_maximum_fusion.2), channel_id=1, source_target_pairs={{0,4},{4,8},{8,12},{12,0},{1,5},{5,9},{9,13},{13,1},{2,6},{6,10},{... | collective-permute-start | bytes 442376 | tf_op jit(solution)/shard_map/ppermute | solution.py:17
  272.8 14.4 %collective-permute-start.18 = (f32[2,48,1,1,128]{4,3,2,1,0:T(1,128)S(1)}, f32[2,48,1,1,128]{4,3,2,1,0:T(1,128)S(1)}, u32[]{:S(2)}, u32[]{:S(2)}) collective-permute-start(f32[2,48,1,1,128]{4,3,2,1,0:T(1,128)S(1)} %fusion.263), channel_id=1, source_target_pairs={{16,0},{0,16},{17,1},{1,17},{18,2},{2,18},{19,3},{3,19},{20,4},{4,... | collective-permute-start | bytes 147464 | tf_op jit(solution)/shard_map/ppermute | solution.py:19
  275.2 12.1 %collective-permute-start.19 = (f32[2,48,1,1,128]{4,3,2,1,0:T(1,128)S(1)}, f32[2,48,1,1,128]{4,3,2,1,0:T(1,128)S(1)}, u32[]{:S(2)}, u32[]{:S(2)}) collective-permute-start(f32[2,48,1,1,128]{4,3,2,1,0:T(1,128)S(1)} %fusion.263), channel_id=1, source_target_pairs={{0,16},{16,0},{1,17},{17,1},{2,18},{18,2},{3,19},{19,3},{4,20},{20... | collective-permute-start | bytes 147464 | tf_op jit(solution)/shard_map/ppermute | solution.py:17
  275.5 7.7 %collective-permute-start.22 = (f32[2,48,1,1,16]{4,3,2,1,0:T(1,128)S(1)}, f32[2,48,1,1,16]{4,3,2,1,0:T(1,128)S(1)}, u32[]{:S(2)}, u32[]{:S(2)}) collective-permute-start(f32[2,48,1,1,16]{4,3,2,1,0:T(1,128)S(1)} %get-tuple-element.797), channel_id=1, source_target_pairs={{1,0},{2,1},{3,2},{0,3},{5,4},{6,5},{7,6},{4,7},{9,8},{10,9},{11,1... | collective-permute-start | bytes 18440 | tf_op jit(solution)/shard_map/ppermute | solution.py:19
  275.6 7.6 %collective-permute-start.23 = (f32[2,48,1,1,16]{4,3,2,1,0:T(1,128)S(1)}, f32[2,48,1,1,16]{4,3,2,1,0:T(1,128)S(1)}, u32[]{:S(2)}, u32[]{:S(2)}) collective-permute-start(f32[2,48,1,1,16]{4,3,2,1,0:T(1,128)S(1)} %get-tuple-element.796), channel_id=1, source_target_pairs={{0,1},{1,2},{2,3},{3,0},{4,5},{5,6},{6,7},{7,4},{8,9},{9,10},{10,1... | collective-permute-start | bytes 18440 | tf_op jit(solution)/shard_map/ppermute | solution.py:17
  287.4 5.9 %collective-permute-start.20 = (f32[2,48,3,1,128]{4,3,2,1,0:T(1,128)S(1)}, f32[2,48,3,1,128]{4,3,2,1,0:T(1,128)S(1)}, u32[]{:S(2)}, u32[]{:S(2)}) collective-permute-start(f32[2,48,3,1,128]{4,3,2,1,0:T(1,128)S(1)} %pad_maximum_fusion.3), channel_id=1, source_target_pairs={{4,0},{8,4},{12,8},{0,12},{5,1},{9,5},{13,9},{1,13},{6,2},{10,6},{... | collective-permute-start | bytes 442376 | tf_op jit(solution)/shard_map/ppermute | solution.py:19
  289.5 8.5 %collective-permute-start.21 = (f32[2,48,3,1,128]{4,3,2,1,0:T(1,128)S(1)}, f32[2,48,3,1,128]{4,3,2,1,0:T(1,128)S(1)}, u32[]{:S(2)}, u32[]{:S(2)}) collective-permute-start(f32[2,48,3,1,128]{4,3,2,1,0:T(1,128)S(1)} %pad_maximum_fusion.3), channel_id=1, source_target_pairs={{0,4},{4,8},{8,12},{12,0},{1,5},{5,9},{9,13},{13,1},{2,6},{6,10},{... | collective-permute-start | bytes 442376 | tf_op jit(solution)/shard_map/ppermute | solution.py:17
  358.5 14.2 %collective-permute-start.24 = (f32[2,48,1,1,128]{4,3,2,1,0:T(1,128)S(1)}, f32[2,48,1,1,128]{4,3,2,1,0:T(1,128)S(1)}, u32[]{:S(2)}, u32[]{:S(2)}) collective-permute-start(f32[2,48,1,1,128]{4,3,2,1,0:T(1,128)S(1)} %fusion.246), channel_id=1, source_target_pairs={{16,0},{0,16},{17,1},{1,17},{18,2},{2,18},{19,3},{3,19},{20,4},{4,... | collective-permute-start | bytes 147464 | tf_op jit(solution)/shard_map/ppermute | solution.py:19
  360.8 11.8 %collective-permute-start.25 = (f32[2,48,1,1,128]{4,3,2,1,0:T(1,128)S(1)}, f32[2,48,1,1,128]{4,3,2,1,0:T(1,128)S(1)}, u32[]{:S(2)}, u32[]{:S(2)}) collective-permute-start(f32[2,48,1,1,128]{4,3,2,1,0:T(1,128)S(1)} %fusion.246), channel_id=1, source_target_pairs={{0,16},{16,0},{1,17},{17,1},{2,18},{18,2},{3,19},{19,3},{4,20},{20... | collective-permute-start | bytes 147464 | tf_op jit(solution)/shard_map/ppermute | solution.py:17
  361.2 7.4 %collective-permute-start.28 = (f32[2,48,1,1,16]{4,3,2,1,0:T(1,128)S(1)}, f32[2,48,1,1,16]{4,3,2,1,0:T(1,128)S(1)}, u32[]{:S(2)}, u32[]{:S(2)}) collective-permute-start(f32[2,48,1,1,16]{4,3,2,1,0:T(1,128)S(1)} %get-tuple-element.763), channel_id=1, source_target_pairs={{1,0},{2,1},{3,2},{0,3},{5,4},{6,5},{7,6},{4,7},{9,8},{10,9},{11,1... | collective-permute-start | bytes 18440 | tf_op jit(solution)/shard_map/ppermute | solution.py:19
  361.2 7.3 %collective-permute-start.29 = (f32[2,48,1,1,16]{4,3,2,1,0:T(1,128)S(1)}, f32[2,48,1,1,16]{4,3,2,1,0:T(1,128)S(1)}, u32[]{:S(2)}, u32[]{:S(2)}) collective-permute-start(f32[2,48,1,1,16]{4,3,2,1,0:T(1,128)S(1)} %get-tuple-element.762), channel_id=1, source_target_pairs={{0,1},{1,2},{2,3},{3,0},{4,5},{5,6},{6,7},{7,4},{8,9},{9,10},{10,1... | collective-permute-start | bytes 18440 | tf_op jit(solution)/shard_map/ppermute | solution.py:17
  372.8 5.9 %collective-permute-start.26 = (f32[2,48,3,1,128]{4,3,2,1,0:T(1,128)S(1)}, f32[2,48,3,1,128]{4,3,2,1,0:T(1,128)S(1)}, u32[]{:S(2)}, u32[]{:S(2)}) collective-permute-start(f32[2,48,3,1,128]{4,3,2,1,0:T(1,128)S(1)} %pad_maximum_fusion.4), channel_id=1, source_target_pairs={{4,0},{8,4},{12,8},{0,12},{5,1},{9,5},{13,9},{1,13},{6,2},{10,6},{... | collective-permute-start | bytes 442376 | tf_op jit(solution)/shard_map/ppermute | solution.py:19
  374.9 8.3 %collective-permute-start.27 = (f32[2,48,3,1,128]{4,3,2,1,0:T(1,128)S(1)}, f32[2,48,3,1,128]{4,3,2,1,0:T(1,128)S(1)}, u32[]{:S(2)}, u32[]{:S(2)}) collective-permute-start(f32[2,48,3,1,128]{4,3,2,1,0:T(1,128)S(1)} %pad_maximum_fusion.4), channel_id=1, source_target_pairs={{0,4},{4,8},{8,12},{12,0},{1,5},{5,9},{9,13},{13,1},{2,6},{6,10},{... | collective-permute-start | bytes 442376 | tf_op jit(solution)/shard_map/ppermute | solution.py:17
  534.4 12.1 %copy-start.1 = (f32[2,48,1,1,128]{4,3,2,1,0:T(1,128)}, f32[2,48,1,1,128]{4,3,2,1,0:T(1,128)S(1)}, u32[]{:S(2)}) copy-start(f32[2,48,1,1,128]{4,3,2,1,0:T(1,128)S(1)} %maximum_add_fusion.11) | copy-start | bytes 147460
  535.3 11.2 %collective-permute-start.30 = (f32[2,48,1,1,128]{4,3,2,1,0:T(1,128)S(1)}, f32[2,48,1,1,128]{4,3,2,1,0:T(1,128)S(1)}, u32[]{:S(2)}, u32[]{:S(2)}) collective-permute-start(f32[2,48,1,1,128]{4,3,2,1,0:T(1,128)S(1)} %maximum_add_fusion.11), channel_id=1, source_target_pairs={{16,0},{0,16},{17,1},{1,17},{18,2},{2,18},{19,3},{3,19},{20,4},{4,... | collective-permute-start | bytes 147464 | tf_op jit(solution)/shard_map/ppermute | solution.py:19
  537.7 8.8 %collective-permute-start.31 = (f32[2,48,1,1,128]{4,3,2,1,0:T(1,128)S(1)}, f32[2,48,1,1,128]{4,3,2,1,0:T(1,128)S(1)}, u32[]{:S(2)}, u32[]{:S(2)}) collective-permute-start(f32[2,48,1,1,128]{4,3,2,1,0:T(1,128)S(1)} %maximum_add_fusion.11), channel_id=1, source_target_pairs={{0,16},{16,0},{1,17},{17,1},{2,18},{18,2},{3,19},{19,3},{4,20},{20... | collective-permute-start | bytes 147464 | tf_op jit(solution)/shard_map/ppermute | solution.py:17
  538.0 1.8 collective-permute-start.34
  538.1 4.3 collective-permute-start.35
  546.7 6.0 %collective-permute-start.32 = (f32[2,48,3,1,128]{4,3,2,1,0:T(1,128)S(1)}, f32[2,48,3,1,128]{4,3,2,1,0:T(1,128)S(1)}, u32[]{:S(2)}, u32[]{:S(2)}) collective-permute-start(f32[2,48,3,1,128]{4,3,2,1,0:T(1,128)S(1)} %pad_maximum_fusion.5), channel_id=1, source_target_pairs={{4,0},{8,4},{12,8},{0,12},{5,1},{9,5},{13,9},{1,13},{6,2},{10,6},{... | collective-permute-start | bytes 442376 | tf_op jit(solution)/shard_map/ppermute | solution.py:19
  548.4 7.9 %collective-permute-start.33 = (f32[2,48,3,1,128]{4,3,2,1,0:T(1,128)S(1)}, f32[2,48,3,1,128]{4,3,2,1,0:T(1,128)S(1)}, u32[]{:S(2)}, u32[]{:S(2)}) collective-permute-start(f32[2,48,3,1,128]{4,3,2,1,0:T(1,128)S(1)} %pad_maximum_fusion.5), channel_id=1, source_target_pairs={{0,4},{4,8},{8,12},{12,0},{1,5},{5,9},{9,13},{13,1},{2,6},{6,10},{... | collective-permute-start | bytes 442376 | tf_op jit(solution)/shard_map/ppermute | solution.py:17
where the time goes:
time: 573 us; the launch traced here: 562 us
  blocking collectives  240 us (42%)
  other arithmetic  112 us (20%)
  between operations  88.9 us (16%)
  local copies, waits for them, and re-layouts  52.9 us (9%)
  waiting for transfers between devices  35.3 us (6%)
  starting transfers between devices  32.3 us (6%)
    psum x5, blocking collectives, per_device(): lax.psum((jnp.stack([entry[0] for entry in local_pairs]), jnp.stack([entr...  198 us
    reduce_sum x24, other arithmetic, block_apply(): real_part = jnp.sum(real_blocks * vec_real - imag_blocks * vec_imag, axis=1)  65.3 us
    psum x1, blocking collectives, per_device(): norm_sq = lax.psum(complex_dot(source, source)[0], ('ta', 'gz', 'xy'))  42.2 us
    ppermute x18, waiting for transfers between devices, padded_2(): lax.ppermute(tail, axis, [(i, (i + 1) % count) for i in range(count)])  28.5 us
    ppermute x18, starting transfers between devices, padded_2(): lax.ppermute(head, axis, [((i + 1) % count, i) for i in range(count)])  26.5 us
    scatter x30, local copies, waits for them, and re-layouts, per_device(): hessenberg.at[0, i, j].set(proj_reals[i]).at[1, i, j].set(proj_imags[i])  25.8 us
    sub x15, other arithmetic, scaled(): coef_real * vector[0] - coef_imag * vector[1]  13.2 us
  transfers between devices with their start and end apart: 36, of which 16 were waited for; matrix products, arithmetic and copies ran while one was open for 12% of the time, Pallas kernels for 0%

commit v1 on v0

v1 whole, which is shorter than its diff:
```python
import functools

import jax
import jax.numpy as jnp
from jax import lax
from jax.experimental import pallas as pl
from jax.experimental.pallas import tpu as pltpu
from jax.sharding import PartitionSpec as P

LY = 16
ITERS = 5
SUB = 8
MESH = pl.DeviceIdType.MESH
ARRIVAL = (6, 7, 4, 5, 0, 1, 2, 3)


def cmul(a, b):
    return (a[0] * b[0] - a[1] * b[1], a[0] * b[1] + a[1] * b[0])


def cmul_conj(a, b):
    return (a[0] * b[0] + a[1] * b[1], a[0] * b[1] - a[1] * b[0])


def csub(a, b):
    return (a[0] - b[0], a[1] - b[1])


def cscale(a, s):
    return (a[0] * s, a[1] * s)


def kernel(sizes, source_hbm, inverse_hbm, links_hbm, sol_ref, res_ref, hes_ref,
           stage, mat_a, mat_b, mat_s, vecs, acc, src, fields, vs, qs,
           halo_t, halo_z, halo_x, pack, red_one, red_two, row_one, row_two,
           load_sem, src_sem, t_send, t_recv, z_send, z_recv, x_send, x_recv,
           one_send, one_recv, two_send, two_recv):
    n_ta, n_gz, n_xy = sizes
    comp, lanes = src.shape[1], src.shape[2]
    tiles = comp // SUB
    me_ta, me_gz, me_xy = (lax.axis_index(a) for a in ("ta", "gz", "xy"))
    n_two = n_ta * n_gz
    me_two = me_ta * n_gz + me_gz

    pltpu.make_async_copy(source_hbm, src, src_sem).start()
    loads = []
    for d in ARRIVAL:
        loads.append(pltpu.make_async_copy(links_hbm.at[d], stage.at[d], load_sem.at[d]))
    loads.append(pltpu.make_async_copy(inverse_hbm, stage.at[8], load_sem.at[8]))
    for load in loads:
        load.start()

    def two_peer(k):
        p = lax.rem(me_two + k, n_two)
        return p, {"ta": p // n_gz, "gz": lax.rem(p, n_gz)}

    barrier = pltpu.get_barrier_semaphore()
    for k in range(1, n_xy):
        pl.semaphore_signal(barrier, inc=1, device_id={"xy": lax.rem(me_xy + k, n_xy)}, device_id_type=MESH)
    for k in range(1, n_two):
        pl.semaphore_signal(barrier, inc=1, device_id=two_peer(k)[1], device_id_type=MESH)
    pltpu.make_async_copy(source_hbm, src, src_sem).wait()
    pl.semaphore_wait(barrier, n_xy - 1 + n_two - 1)

    lane = lax.broadcasted_iota(jnp.int32, (SUB, lanes), 1)
    lane_all = lax.broadcasted_iota(jnp.int32, (comp, lanes), 1)
    pending = []

    def remote(s, d, send, recv, device):
        return pltpu.make_async_remote_copy(
            src_ref=s, dst_ref=d, send_sem=send, recv_sem=recv, device_id=device, device_id_type=MESH)

    def packed(value, first):
        out = jnp.zeros((SUB, lanes), jnp.float32)
        for k in range(tiles):
            tile = value[k * SUB:(k + 1) * SUB]
            shift = (LY * k + (0 if first else LY)) % lanes
            if shift:
                tile = pltpu.roll(tile, shift, 1)
            out = jnp.where(lane // LY == k, tile, out)
        return out

    def unpacked(value, first):
        out = []
        for k in range(tiles):
            shift = ((0 if first else lanes - LY) - LY * k) % lanes
            out.append(pltpu.roll(value, shift, 1) if shift else value)
        return jnp.concatenate(out, axis=0)

    def send_halo(e, ref):
        for c in range(2):
            value = ref[c]
            pack[e, 0, c] = packed(value, True)
            pack[e, 1, c] = packed(value, False)
        waits = {}
        for slot, step in ((0, n_xy - 1), (1, 1)):
            cp = remote(pack.at[e, slot], halo_x.at[e, slot], x_send.at[e, slot], x_recv.at[e, slot],
                        {"xy": lax.rem(me_xy + step, n_xy)})
            cp.start()
            pending.append(cp)
            waits["x", slot] = cp
        for slot, step in ((0, n_gz - 1), (1, 1)):
            cp = remote(ref, halo_z.at[e, slot], z_send.at[e, slot], z_recv.at[e, slot],
                        {"gz": lax.rem(me_gz + step, n_gz)})
            cp.start()
            pending.append(cp)
            waits["z", slot] = cp
        for slot, step in ((0, n_ta - 1), (1, 1))[:1 if n_ta == 2 else 2]:
            cp = remote(ref, halo_t.at[e, slot], t_send.at[e, slot], t_recv.at[e, slot],
                        {"ta": lax.rem(me_ta + step, n_ta)})
            cp.start()
            pending.append(cp)
            waits["t", slot] = cp
        return waits

    def put(slot, re, im):
        vecs[slot, 0] = re
        vecs[slot, 1] = im - re
        vecs[slot, 2] = re + im

    def set_y(ref):
        pos = lane_all % LY
        fwd, bwd = [], []
        for c in range(2):
            v = ref[c]
            fwd.append(jnp.where(pos == LY - 1, pltpu.roll(v, LY - 1, 1), pltpu.roll(v, lanes - 1, 1)))
            bwd.append(jnp.where(pos == 0, pltpu.roll(v, lanes - LY + 1, 1), pltpu.roll(v, 1, 1)))
        put(6, *fwd)
        put(7, *bwd)

    def set_x(e, ref, waits):
        fwd, bwd = [], []
        waits["x", 0].wait_recv()
        waits["x", 1].wait_recv()
        for c in range(2):
            v = ref[c]
            fwd.append(jnp.where(lane_all >= lanes - LY, unpacked(halo_x[e, 0, c], False), pltpu.roll(v, lanes - LY, 1)))
            bwd.append(jnp.where(lane_all < LY, unpacked(halo_x[e, 1, c], True), pltpu.roll(v, LY, 1)))
        put(4, *fwd)
        put(5, *bwd)

    def set_t(e, waits):
        waits["t", 0].wait_recv()
        put(0, halo_t[e, 0, 0], halo_t[e, 0, 1])
        back = 0
        if n_ta != 2:
            waits["t", 1].wait_recv()
            back = 1
        put(1, halo_t[e, back, 0], halo_t[e, back, 1])

    def set_z(e, waits):
        for slot in range(2):
            waits["z", slot].wait_recv()
            put(2 + slot, halo_z[e, slot, 0], halo_z[e, slot, 1])

    def convert(d):
        def body(i, _):
            rows = pl.ds(i * 2, 2)
            a = stage[d, 0, rows].astype(jnp.float32)
            b = stage[d, 1, rows].astype(jnp.float32)
            mat_a[d, rows] = a
            mat_b[d, rows] = b
            mat_s[d, rows] = a + b
            return 0

        lax.fori_loop(0, comp // 2, body, 0)

    def products(dirs, first, out=None):
        def body(b, _):
            rows = pl.ds(b * SUB, SUB)
            if first:
                sums = [jnp.zeros((SUB, SUB, lanes), jnp.float32)] * 3
            else:
                sums = [acc[m, rows] for m in range(3)]
            for d in dirs:
                slot = 0 if d == 8 else d
                for k in range(tiles):
                    cols = pl.ds(k * SUB, SUB)
                    for m, mat in enumerate((mat_s, mat_a, mat_b)):
                        sums[m] = sums[m] + mat[d, rows, cols] * vecs[slot, m, cols][None]
            if out is None:
                for m in range(3):
                    acc[m, rows] = sums[m]
            else:
                out[0, rows] = jnp.sum(sums[0] - sums[2], axis=1)
                out[1, rows] = jnp.sum(sums[0] + sums[1], axis=1)
            return 0

        lax.fori_loop(0, comp // SUB, body, 0)

    def finish_apply(out):
        put(0, fields[0, 0], fields[0, 1])
        products((8,), True, out)

    row16 = lax.broadcasted_iota(jnp.int32, (2 * SUB, lanes), 0)
    lane16 = lax.broadcasted_iota(jnp.int32, (2 * SUB, lanes), 1)

    def start_reduce(j, values):
        table = jnp.zeros((2 * SUB, lanes), jnp.float32)
        for k, value in enumerate(values):
            table = jnp.where(row16 == k, jnp.sum(value, axis=0, keepdims=True), table)
        table = jnp.sum(table, axis=1, keepdims=True)
        row = jnp.sum(jnp.where(row16 == lane16, table, 0.0), axis=0, keepdims=True)
        row_one[j] = row
        for k in range(1, n_xy):
            cp = remote(row_one.at[j], red_one.at[j, me_xy], one_send.at[j, k], one_recv.at[j, me_xy],
                        {"xy": lax.rem(me_xy + k, n_xy)})
            cp.start()
            pending.append(cp)
        red_one[j, me_xy] = row

    def middle_reduce(j):
        for k in range(1, n_xy):
            p = lax.rem(me_xy + n_xy - k, n_xy)
            remote(row_one.at[j], red_one.at[j, p], one_send.at[j, k], one_recv.at[j, p], {"xy": p}).wait_recv()
        row = red_one[j, 0]
        for k in range(1, n_xy):
            row = row + red_one[j, k]
        row_two[j] = row
        for k in range(1, n_two):
            cp = remote(row_two.at[j], red_two.at[j, me_two], two_send.at[j, k], two_recv.at[j, me_two], two_peer(k)[1])
            cp.start()
            pending.append(cp)
        red_two[j, me_two] = row

    def end_reduce(j, count):
        for k in range(1, n_two):
            p, device = two_peer(n_two - k)
            remote(row_two.at[j], red_two.at[j, p], two_send.at[j, k], two_recv.at[j, p], device).wait_recv()
        row = red_two[j, 0]
        for k in range(1, n_two):
            row = row + red_two[j, k]
        return [jnp.broadcast_to(row[:, k:k + 1], (1, lanes)) for k in range(count)]

    def load(ref):
        return (ref[0], ref[1])

    def store(ref, value):
        ref[0] = value[0]
        ref[1] = value[1]

    def dots(vector_refs, q):
        values = []
        for ref in vector_refs:
            values.extend(cmul_conj(load(ref), q))
        values.append(q[0] * q[0] + q[1] * q[1])
        return values

    waits = send_halo(0, src)
    for at, d in enumerate(ARRIVAL):
        if d == 6:
            set_y(src)
        elif d == 4:
            set_x(0, src, waits)
        elif d == 0:
            set_t(0, waits)
        elif d == 2:
            set_z(0, waits)
        loads[at].wait()
        convert(d)
        products((d,), at == 0, fields.at[0] if at == 7 else None)
    loads[8].wait()
    convert(8)
    raw = fields.at[1]
    finish_apply(raw)

    def apply(e, ref, out, j):
        set_y(ref)
        products((6, 7), True)
        middle_reduce(j)
        set_x(e, ref, waits)
        products((4, 5), False)
        set_t(e, waits)
        set_z(e, waits)
        products((0, 1, 2, 3), False, fields.at[0])
        finish_apply(out)

    waits = send_halo(1, raw)
    source = load(src)
    q = load(raw)
    start_reduce(0, dots([src], q) + [source[0] * source[0] + source[1] * source[1]])
    product = fields.at[2]
    apply(1, raw, product, 0)
    dot_re, dot_im, q_sq, norm_sq = end_reduce(0, 4)
    source_norm = jnp.sqrt(norm_sq)
    scale = 1.0 / source_norm
    store(vs.at[0], cscale(load(src), scale))
    store(qs.at[0], cscale(load(raw), scale))
    store(product, cscale(load(product), scale))
    g = [(dot_re * scale * scale, dot_im * scale * scale)]
    q_sq = q_sq * scale * scale

    columns = []
    low = [[None] * ITERS for _ in range(ITERS)]
    inv_diag, forward = [], []

    def factor_row(j):
        entries = []
        for k in range(j + 1):
            total = cmul_conj(columns[j][0], columns[k][0])
            for m in range(1, k + 2):
                term = cmul_conj(columns[j][m], columns[k][m])
                total = (total[0] + term[0], total[1] + term[1])
            entries.append(total)
        for k in range(j):
            total = entries[k]
            for m in range(k):
                total = csub(total, cmul_conj(low[k][m], low[j][m]))
            low[j][k] = cscale(total, inv_diag[k])
        diag = entries[j][0]
        for m in range(j):
            diag = diag - (low[j][m][0] * low[j][m][0] + low[j][m][1] * low[j][m][1])
        inv_diag.append(1.0 / jnp.sqrt(diag))
        total = (source_norm * columns[j][0][0], -source_norm * columns[j][0][1])
        for m in range(j):
            total = csub(total, cmul(low[j][m], forward[m]))
        forward.append(cscale(total, inv_diag[j]))

    zero = jnp.zeros((1, lanes), jnp.float32)
    for j in range(ITERS):
        length_sq = q_sq
        for re, im in g:
            length_sq = length_sq - (re * re + im * im)
        length = jnp.sqrt(length_sq)
        columns.append(g[:j] + [(g[j][0] + 1.0, g[j][1]), (length, zero)])
        if j < ITERS - 1:
            scale = 1.0 / length
            v = load(qs.at[j])
            q = load(product)
            for i in range(j + 1):
                v = csub(v, cmul(g[i], load(vs.at[i])))
                q = csub(q, cmul(g[i], load(qs.at[i])))
            store(qs.at[j + 1], cscale(q, scale))
            store(vs.at[j + 1], cscale(v, scale))
            last = j + 1 == ITERS - 1
            if not last:
                waits = send_halo(j + 2, qs.at[j + 1])
            start_reduce(j + 1, dots([vs.at[i] for i in range(j + 2)], load(qs.at[j + 1])))
            factor_row(j)
            if last:
                middle_reduce(j + 1)
            else:
                product = fields.at[j + 3]
                apply(j + 2, qs.at[j + 1], product, j + 1)
            got = end_reduce(j + 1, 2 * (j + 2) + 1)
            g = [(got[2 * i], got[2 * i + 1]) for i in range(j + 2)]
            q_sq = got[2 * (j + 2)]
        else:
            factor_row(j)

    coeffs = [None] * ITERS
    for j in reversed(range(ITERS)):
        total = forward[j]
        for m in range(j + 1, ITERS):
            total = csub(total, cmul_conj(low[m][j], coeffs[m]))
        coeffs[j] = cscale(total, inv_diag[j])

    answer = cmul(coeffs[0], load(vs.at[0]))
    left = csub(load(src), cmul(coeffs[0], load(qs.at[0])))
    for j in range(1, ITERS):
        term = cmul(coeffs[j], load(vs.at[j]))
        answer = (answer[0] + term[0], answer[1] + term[1])
        left = csub(left, cmul(coeffs[j], load(qs.at[j])))
    store(sol_ref, answer)
    store(res_ref, csub(left, answer))

    shape = hes_ref.shape[1:]
    row = lax.broadcasted_iota(jnp.int32, shape, 0)
    col = lax.broadcasted_iota(jnp.int32, shape, 1)
    for c in range(2):
        table = jnp.zeros(shape, jnp.float32)
        for j in range(ITERS):
            for i in range(j + 2):
                table = jnp.where((row == i) & (col == j), columns[j][i][c][:, :shape[1]], table)
        hes_ref[c] = table

    for cp in pending:
        cp.wait_send()


def solution(mesh):
    sizes = tuple(mesh.shape[a] for a in ("ta", "gz", "xy"))

    def per_device(source, inverse, coarse_links):
        comp, lanes = source.shape[1], source.shape[4]
        f32 = jnp.float32
        field = (2, comp, lanes)
        mats = (9, comp, comp, lanes)
        n_two = sizes[0] * sizes[1]
        dma = pltpu.SemaphoreType.DMA
        hbm = pl.BlockSpec(memory_space=pl.ANY)
        vmem = pl.BlockSpec(memory_space=pltpu.VMEM)
        sol, res, hes = pl.pallas_call(
            functools.partial(kernel, sizes),
            out_shape=(
                jax.ShapeDtypeStruct(field, f32),
                jax.ShapeDtypeStruct(field, f32),
                jax.ShapeDtypeStruct((2, ITERS + 1, ITERS), f32),
            ),
            in_specs=[hbm, hbm, hbm],
            out_specs=(vmem, vmem, vmem),
            scratch_shapes=[
                pltpu.VMEM((9, 2, comp, comp, lanes), coarse_links.dtype),
                pltpu.VMEM(mats, f32),
                pltpu.VMEM(mats, f32),
                pltpu.VMEM(mats, f32),
                pltpu.VMEM((8, 3, comp, lanes), f32),
                pltpu.VMEM((3, comp, SUB, lanes), f32),
                pltpu.VMEM(field, f32),
                pltpu.VMEM((ITERS + 1, *field), f32),
                pltpu.VMEM((ITERS, *field), f32),
                pltpu.VMEM((ITERS, *field), f32),
                pltpu.VMEM((ITERS, 2, *field), f32),
                pltpu.VMEM((ITERS, 2, *field), f32),
                pltpu.VMEM((ITERS, 2, 2, SUB, lanes), f32),
                pltpu.VMEM((ITERS, 2, 2, SUB, lanes), f32),
                pltpu.VMEM((ITERS, sizes[2], 1, lanes), f32),
                pltpu.VMEM((ITERS, n_two, 1, lanes), f32),
                pltpu.VMEM((ITERS, 1, lanes), f32),
                pltpu.VMEM((ITERS, 1, lanes), f32),
                dma((9,)),
                dma,
                dma((ITERS, 2)), dma((ITERS, 2)),
                dma((ITERS, 2)), dma((ITERS, 2)),
                dma((ITERS, 2)), dma((ITERS, 2)),
                dma((ITERS, sizes[2])), dma((ITERS, sizes[2])),
                dma((ITERS, n_two)), dma((ITERS, n_two)),
            ],
            compiler_params=pltpu.CompilerParams(
                collective_id=0, has_side_effects=True, vmem_limit_bytes=60 * 1024 * 1024),
        )(
            source.reshape(field),
            inverse.reshape(2, comp, comp, lanes),
            coarse_links.reshape(8, 2, comp, comp, lanes),
        )
        return sol.reshape(source.shape), res.reshape(source.shape), hes

    specs = (
        P(None, None, "ta", "gz", "xy"),
        P(None, None, None, "ta", "gz", "xy"),
        P(None, None, None, None, "ta", "gz", "xy"),
    )
    return jax.shard_map(
        per_device,
        mesh=mesh,
        in_specs=specs,
        out_specs=(specs[0], specs[0], P()),
        check_vma=False,
    )
```

time: 573 us -> 55.5 us (0.10); the launches traced: 562 us -> 55.3 us
  blocking collectives: 240 us -> 0 us
  other arithmetic: 112 us -> 0 us
  between operations: 88.9 us -> 0.64 us
  Pallas kernels: 0 us -> 50.4 us
  local copies, waits for them, and re-layouts: 52.9 us -> 4.22 us
  waiting for transfers between devices: 35.3 us -> 0 us
  starting transfers between devices: 32.3 us -> 0 us
    psum x6 -> x0, blocking collectives: 240 us -> none  [the longest x5 198 us: per_device(): lax.psum((jnp.stack([entry[0] for entry in local_pairs]), jnp.stack([entr...]
    reduce_sum x34 -> x0, other arithmetic: 73.8 us -> none  [the longest x24 65.3 us: block_apply(): real_part = jnp.sum(real_blocks * vec_real - imag_blocks * vec_imag, axis=1)]
    pallas_call x0 -> x1, Pallas kernels: none -> 50.4 us  [per_device(): pl.pallas_call(functools.partial(kernel, sizes), out_shape=(jax.ShapeDtyp...]
    ppermute x36 -> x0, waiting for transfers between devices: 35.3 us -> none  [the longest x18 28.5 us: padded_2(): lax.ppermute(tail, axis, [(i, (i + 1) % count) for i in range(count)])]
    ppermute x36 -> x0, starting transfers between devices: 32.3 us -> none  [the longest x18 26.5 us: padded_2(): lax.ppermute(head, axis, [((i + 1) % count, i) for i in range(count)])]
    scatter x35 -> x0, local copies, waits for them, and re-layouts: 27.7 us -> none  [the longest x30 25.8 us: per_device(): hessenberg.at[0, i, j].set(proj_reals[i]).at[1, i, j].set(proj_imags[i])]
    another operation x11 -> x0, other arithmetic: 14.1 us -> none  [the longest x3 5.9 us: per_device(): jnp.stack([entry[1] for entry in local_pairs])]
    sub x16 -> x0, other arithmetic: 14 us -> none  [the longest x15 13.2 us: scaled(): coef_real * vector[0] - coef_imag * vector[1]]
  transfers between devices with their start and end apart: 36 -> 0, of which waited for: 16 -> 0; matrix products, arithmetic and copies ran while one was open for 12% -> 0% of each run, Pallas kernels for 0% -> 0%
where the time goes in v1:
time: 55.5 us; the launch traced here: 55.3 us
  Pallas kernels  50.4 us (91%)
  local copies, waits for them, and re-layouts  4.22 us (8%)
  between operations  0.64 us (1%)
    pallas_call x1, Pallas kernels, per_device(): pl.pallas_call(functools.partial(kernel, sizes), out_shape=(jax.ShapeDtyp...  50.4 us
    unnamed x3, local copies, waits for them, and re-layouts  4.22 us

profile of v1, /device:TPU:0, one launch (start us, length us, event | category | flops | bytes accessed | tf_op | source)
XLA Modules:
  0.0 55.3 jit_solution(15482427921135294963)
XLA Ops:
  0.6 50.4 %shard_map.58 = (f32[2,48,128]{2,1,0:T(8,128)}, f32[2,48,128]{2,1,0:T(8,128)}, f32[2,6,5]{2,1,0:T(8,128)}) custom-call(f32[2,48,128]{2,1,0:T(8,128)} %bitcast.11, bf16[2,48,48,128]{3,2,1,0:T(8,128)(2,1)} %bitcast.10, bf16[8,2,48,48,128]{4,3,2,1,0:T(8,128)(2,1)} %bitcast.9), custom_call_target="tpu_custom_call" | custom-call | tf_op jit(solution)/shard_map/pallas_call | solution.py:393
  51.1 1.4 %copy.8 = f32[2,6,5]{1,0,2:T(2,128)} copy(f32[2,6,5]{2,1,0:T(8,128)} %get-tuple-element.11) | data formatting | bytes 480
  52.4 1.4 %copy.11 = f32[2,48,1,1,128]{4,3,2,1,0:T(1,128)} copy(f32[2,48,1,1,128]{4,3,2,1,0:T(1,128)} %bitcast.13) | data formatting | bytes 98304
  53.9 1.4 %copy.12 = f32[2,48,1,1,128]{4,3,2,1,0:T(1,128)} copy(f32[2,48,1,1,128]{4,3,2,1,0:T(1,128)} %bitcast.12) | data formatting | bytes 98304

commit v2 on v1

--- a/solution.py
+++ b/solution.py
@@ -275,10 +275,10 @@
         products((0, 1, 2, 3), False, fields.at[0])
         finish_apply(out)
 
-    waits = send_halo(1, raw)
     source = load(src)
     q = load(raw)
     start_reduce(0, dots([src], q) + [source[0] * source[0] + source[1] * source[1]])
+    waits = send_halo(1, raw)
     product = fields.at[2]
     apply(1, raw, product, 0)
     dot_re, dot_im, q_sq, norm_sq = end_reduce(0, 4)
@@ -333,9 +333,9 @@
             store(qs.at[j + 1], cscale(q, scale))
             store(vs.at[j + 1], cscale(v, scale))
             last = j + 1 == ITERS - 1
+            start_reduce(j + 1, dots([vs.at[i] for i in range(j + 2)], load(qs.at[j + 1])))
             if not last:
                 waits = send_halo(j + 2, qs.at[j + 1])
-            start_reduce(j + 1, dots([vs.at[i] for i in range(j + 2)], load(qs.at[j + 1])))
             factor_row(j)
             if last:
                 middle_reduce(j + 1)
@@ -365,17 +365,23 @@
     store(res_ref, csub(left, answer))
 
     shape = hes_ref.shape[1:]
-    row = lax.broadcasted_iota(jnp.int32, shape, 0)
-    col = lax.broadcasted_iota(jnp.int32, shape, 1)
-    for c in range(2):
+    part = lax.broadcasted_iota(jnp.int32, shape, 0)
+    row = lax.broadcasted_iota(jnp.int32, shape, 1)
+    for j in range(ITERS):
         table = jnp.zeros(shape, jnp.float32)
-        for j in range(ITERS):
-            for i in range(j + 2):
-                table = jnp.where((row == i) & (col == j), columns[j][i][c][:, :shape[1]], table)
-        hes_ref[c] = table
+        for i in range(j + 2):
+            re, im = (x[:, :shape[1]] for x in columns[j][i])
+            table = jnp.where(row == i, jnp.where(part == 0, re, im), table)
+        hes_ref[j] = table
 
     for cp in pending:
         cp.wait_send()
+
+
+def hand_on(*refs):
+    half = len(refs) // 2
+    for i in range(half):
+        refs[half + i][...] = refs[i][...]
 
 
 def solution(mesh):
@@ -395,7 +401,7 @@
             out_shape=(
                 jax.ShapeDtypeStruct(field, f32),
                 jax.ShapeDtypeStruct(field, f32),
-                jax.ShapeDtypeStruct((2, ITERS + 1, ITERS), f32),
+                jax.ShapeDtypeStruct((ITERS, 2, ITERS + 1), f32),
             ),
             in_specs=[hbm, hbm, hbm],
             out_specs=(vmem, vmem, vmem),
@@ -433,7 +439,14 @@
             inverse.reshape(2, comp, comp, lanes),
             coarse_links.reshape(8, 2, comp, comp, lanes),
         )
-        return sol.reshape(source.shape), res.reshape(source.shape), hes
+        results = (sol, res, hes)
+        sol, res, hes = pl.pallas_call(
+            hand_on,
+            out_shape=tuple(jax.ShapeDtypeStruct(x.shape, x.dtype) for x in results),
+            in_specs=[vmem] * 3,
+            out_specs=(vmem,) * 3,
+        )(*results)
+        return sol.reshape(source.shape), res.reshape(source.shape), hes.transpose(1, 2, 0)
 
     specs = (
         P(None, None, "ta", "gz", "xy"),

time: 55.5 us -> 52.5 us (0.946)
  local copies, waits for them, and re-layouts: 4.22 us -> 0 us
  Pallas kernels: 50.4 us -> 51.7 us
    unnamed x3 -> x0, local copies, waits for them, and re-layouts: 4.22 us -> none
    pallas_call x0 -> x1, Pallas kernels: none -> 1.47 us  [per_device(): pl.pallas_call(hand_on, out_shape=tuple((jax.ShapeDtypeStruct(x.shape, x....]
where the time goes in v2:
time: 52.5 us; the launch traced here: 52.3 us
  Pallas kernels  51.7 us (98%)
  between operations  0.64 us (1%)
    pallas_call x1, Pallas kernels, per_device(): pl.pallas_call(functools.partial(kernel, sizes), out_shape=(jax.ShapeDtyp...  50.2 us
    pallas_call x1, Pallas kernels, per_device(): pl.pallas_call(hand_on, out_shape=tuple((jax.ShapeDtypeStruct(x.shape, x....  1.47 us

profile of v2, /device:TPU:0, one launch (start us, length us, event | category | flops | bytes accessed | tf_op | source)
XLA Modules:
  0.0 52.3 jit_solution(9163087961424775248)
XLA Ops:
  0.6 50.2 %shard_map.58 = (f32[2,48,128]{2,1,0:T(8,128)}, f32[2,48,128]{2,1,0:T(8,128)}, f32[5,2,6]{2,1,0:T(2,128)}) custom-call(f32[2,48,128]{2,1,0:T(8,128)} %bitcast.12, bf16[2,48,48,128]{3,2,1,0:T(8,128)(2,1)} %bitcast.11, bf16[8,2,48,48,128]{4,3,2,1,0:T(8,128)(2,1)} %bitcast.10), custom_call_target="tpu_custom_call" | custom-call | tf_op jit(solution)/shard_map/pallas_call | solution.py:399
  50.8 1.5 %shard_map.59 = (f32[2,48,128]{2,1,0:T(8,128)}, f32[2,48,128]{2,1,0:T(8,128)}, f32[5,2,6]{2,1,0:T(2,128)}) custom-call(f32[2,48,128]{2,1,0:T(8,128)} %get-tuple-element.9.refs_0_, f32[2,48,128]{2,1,0:T(8,128)} %get-tuple-element.10.refs_1_, f32[5,2,6]{2,1,0:T(2,128)} %get-tuple-element.11.refs_2_), custom_call_target="tpu_custom_call" | custom-call | tf_op jit(solution)/shard_map/pallas_call | solution.py:443
